TPU v7x, 32 devices: a whole 2x2x4 slice. The times are simulated.
32 devices in a mesh: heads: 4 (over y, core), batch: 8 (over z, x).
Axes of the slice: x: 2, y: 2, z: 4, core: 2. Of those that a mesh axis runs over, the one named last changes fastest.
Arguments:
- queries: bfloat16 [64, 4096], P('batch', 'heads'), may hold values from -6 to 6
- keys_new: bfloat16 [64, 4096], P('batch', 'heads'), may hold values from -6 to 6
- values_new: bfloat16 [64, 4096], P('batch', 'heads'), may hold values from -6 to 6
- out_gate: bfloat16 [64, 4096], P('batch', 'heads'), may hold values from -6 to 6
- decay_logit: float32 [64, 32], P('batch', 'heads'), may hold values from -6 to 6
- beta_logit: float32 [64, 32], P('batch', 'heads'), may hold values from -6 to 6
- decay_rate: float32 [32], P('heads'), may hold values from 0.05 to 2
- state: float32 [64, 32, 128, 128], P('batch', 'heads'), may hold values from -0.6 to 0.6
- norm_gain: float32 [128], replicated, may hold values from 0.1 to 1.9
- out_proj: bfloat16 [4096, 4096], P('heads'), may hold values from -0.09375 to 0.09375
- residual: bfloat16 [64, 4096], P('batch'), may hold values from -40 to 40, as said below
- final_gain: float32 [4096], replicated, may hold values from 0.1 to 1.9
- value_weight: float32 [4096], replicated, may hold values from -0.09375 to 0.09375
- lm_head: bfloat16 [4096, 4096], P(None, ('heads', 'batch')), may hold values from -15 to 15
- sampled: int32 [64], replicated, may hold values from 0 to 4095
Outputs:
- logprob: float32 [64], P('batch')
- value: float32 [64], P('batch')
Inputs may be any that keep to these rules, and one draw needn't show every extreme that they name: The residual stream's entries have scales that differ by row and by column (up to tenfold each), so neither rows nor columns share one magnitude.
All inputs are finite; a program needn't handle non-finite values.
Results may differ from a plain program's by a relative error of at most 0.0013.
Values may be sent and summed in bfloat16 or wider, within the bound.
A program may use at most 64 MiB of HBM per device.

v0:
```python
import jax
import jax.numpy as jnp
from jax import lax
from jax.sharding import PartitionSpec as P

epsilon = 1e-06


def joined(part, axis, combine):
    gathered = jax.tree.map(lambda a: lax.all_gather(a, axis), part)

    def take(source):
        return jax.tree.map(lambda a: lax.dynamic_index_in_dim(a, source, 0, False), gathered)

    return lax.fori_loop(
        1, lax.axis_size(axis), lambda source, state: combine(state, take(source)), take(0)
    )


def head_outputs(
    queries, keys_new, values_new, out_gate, decay_logit, beta_logit, decay_rate, state, norm_gain
):
    rows_here, heads_here = decay_logit.shape
    query_f = queries.astype(jnp.float32).reshape(rows_here, heads_here, -1)
    key_f = keys_new.astype(jnp.float32).reshape(rows_here, heads_here, -1)
    value_f = values_new.astype(jnp.float32).reshape(rows_here, heads_here, -1)
    gate_f = out_gate.astype(jnp.float32).reshape(rows_here, heads_here, -1)
    key_size = query_f.shape[2]
    query_n = query_f / jnp.sqrt(jnp.sum(query_f * query_f, axis=2, keepdims=True) + epsilon)
    query_n = query_n * key_size ** (-0.5)
    key_n = key_f / jnp.sqrt(jnp.sum(key_f * key_f, axis=2, keepdims=True) + epsilon)
    decay = jnp.exp(-decay_rate[None, :] * jax.nn.softplus(decay_logit))
    strength = jax.nn.sigmoid(beta_logit)
    state_query = jnp.einsum("bhk,bhkv->bhv", query_n, state, precision=lax.Precision.HIGHEST)
    state_key = jnp.einsum("bhk,bhkv->bhv", key_n, state, precision=lax.Precision.HIGHEST)
    intersection = jnp.sum(query_n * key_n, axis=2, keepdims=True)
    written = value_f - decay[..., None] * state_key
    output = decay[..., None] * state_query + strength[..., None] * intersection * written
    normed = output / jnp.sqrt(jnp.mean(output * output, axis=2, keepdims=True) + epsilon)
    result = normed * norm_gain * jax.nn.silu(gate_f)
    return result.reshape(rows_here, -1).astype(jnp.bfloat16)


def merge_stats(earlier, later):
    top = jnp.maximum(earlier[0], later[0])
    total = earlier[1] * jnp.exp(earlier[0] - top) + later[1] * jnp.exp(later[0] - top)
    return (top, total, earlier[2] + later[2])


def per_device(
    queries,
    keys_new,
    values_new,
    out_gate,
    decay_logit,
    beta_logit,
    decay_rate,
    state,
    norm_gain,
    out_proj,
    residual,
    final_gain,
    value_weight,
    lm_head,
    sampled,
):
    headout = head_outputs(
        queries,
        keys_new,
        values_new,
        out_gate,
        decay_logit,
        beta_logit,
        decay_rate,
        state,
        norm_gain,
    )
    partial_out = jnp.dot(headout, out_proj, preferred_element_type=jnp.float32)
    rows_own = residual.shape[0]
    attn = lax.psum(partial_out, "heads")
    hsum = residual.astype(jnp.float32) + attn
    rstd = 1.0 / jnp.sqrt(jnp.mean(hsum * hsum, axis=1) + epsilon)
    value = rstd * jnp.sum(hsum * final_gain * value_weight, axis=1)
    normed = (hsum * rstd[:, None] * final_gain).astype(jnp.bfloat16)
    logits = jnp.dot(
        lax.all_gather(normed, "batch", axis=0, tiled=True),
        lm_head,
        preferred_element_type=jnp.float32,
    )
    vocab_own = lm_head.shape[1]
    vocab_first = lax.axis_index(("heads", "batch")) * vocab_own
    local_ids = sampled - vocab_first
    columns = lax.broadcasted_iota(jnp.int32, logits.shape, 1)
    chosen = jnp.sum(jnp.where(columns == local_ids[:, None], logits, 0.0), axis=1)
    local_top = jnp.max(logits, axis=1)
    local_total = jnp.sum(jnp.exp(logits - local_top[:, None]), axis=1)
    top, total, chosen_all = joined(
        (local_top, local_total, chosen), ("heads", "batch"), merge_stats
    )
    every_logprob = chosen_all - (top + jnp.log(total))
    logprob = lax.dynamic_slice_in_dim(
        every_logprob, lax.axis_index("batch") * rows_own, rows_own, 0
    )
    return (logprob, value)


def solution(mesh):
    placed = (
        P("batch", "heads"),
        P("batch", "heads"),
        P("batch", "heads"),
        P("batch", "heads"),
        P("batch", "heads"),
        P("batch", "heads"),
        P("heads"),
        P("batch", "heads", None, None),
        P(),
        P("heads", None),
        P("batch", None),
        P(),
        P(),
        P(None, ("heads", "batch")),
        P(),
    )
    return jax.shard_map(
        per_device, mesh=mesh, in_specs=placed, out_specs=(P("batch"), P("batch")), check_vma=False
    )
```

profile of v0, /device:TPU:0, one launch (start us, length us, event | category | flops | bytes accessed | tf_op | source)
XLA Modules:
  0.0 143.0 jit_solution(5027682328408560421)
XLA Ops:
  7.2 1.0 fusion.7
  8.2 1.1 fusion.9
  9.3 0.9 fusion.22
  10.3 5.3 %fusion.16 = f32[8,8,1,128]{3,2,1,0:T(1,128)S(1)} fusion(f32[8,8,128,128]{3,2,1,0:T(8,128)} %param.24, f32[8,8,128,1]{2,0,1,3:T(8,128)S(1)} %get-tuple-element.209), kind=kOutput, calls=%fused_computation.32 | convolution fusion | flops 12582912 | bytes 4259840 | tf_op jit(solution)/shard_map/bhk,bhkv->bhv/dot_general | solution.py:35
  15.6 3.7 %fusion.18 = f32[8,8,1,128]{3,2,1,0:T(1,128)S(1)} fusion(f32[8,8,128,128]{3,2,1,0:T(8,128)S(1)} %copy-done.1, f32[8,8,128,1]{2,0,1,3:T(8,128)S(1)} %get-tuple-element.207), kind=kOutput, calls=%fused_computation.34 | convolution fusion | flops 12582912 | bytes 4259840 | tf_op jit(solution)/shard_map/bhk,bhkv->bhv/dot_general | solution.py:34
  19.4 0.1 copy.19
  19.5 0.2 multiply_reduce_fusion.2
  19.7 5.3 %fusion.23 = f32[8,4096]{1,0:T(8,128)} fusion(bf16[1024,4096]{1,0:T(8,128)(2,1)} %param.26, bf16[8,1024]{1,0:T(8,128)(2,1)S(1)} %copy-done.5, f32[128]{0:T(128)S(1)} %copy-done.9, f32[8,8]{0,1:T(8,128)S(1)} %add_sqrt_fusion, f32[8,8,1,128]{3,2,1,0:T(1,128)S(1)} %fusion.16, f32[8,8,1,128]{3,2,1,0:T(1,128)S(1)} %fusion.18, bf16[8,1024]{1,0:T(8,128)(2,1)S(1)} %copy-done.3, ...), kind=kOutput, calls=%fused_computation.44 | convolution fusion | flops 67231744 | bytes 8619264 | tf_op jit(solution)/shard_map/dot_general | solution.py:78
  25.1 34.6 %all-reduce.6.cloned.1.call-done = f32[8,4096]{1,0:T(8,128)} async-done(((f32[8,4096]{1,0:T(8,128)}), f32[8,4096]{1,0:T(8,128)}) %all-reduce.6.cloned.1.call-update) | async-done | bytes 131088 | tf_op jit(solution)/shard_map/psum | solution.py:80
  59.7 1.1 multiply_reduce_fusion
  60.8 0.5 fusion.32
  61.4 1.0 multiply_convert_fusion
  62.4 31.4 %all_gather.21 = bf16[64,4096]{1,0:T(8,128)(2,1)S(1)} all-gather(bf16[8,4096]{1,0:T(8,128)(2,1)S(1)} %multiply_convert_fusion), channel_id=1, replica_groups=mesh['heads'=4,'batch'=8] {'batch'}, dimensions={0}, use_global_device_ids=true | all-gather | bytes 589824 | tf_op jit(solution)/shard_map/all_gather | solution.py:86
  93.7 0.4 fusion.35
  94.2 0.2 select_reduce_fusion
  94.4 0.3 dynamic-update-slice
  94.7 0.3 dynamic-update-slice.2
  94.9 0.3 dynamic-update-slice.1
  95.2 38.7 %all-reduce.3 = (f32[2048]{0:T(1024)S(1)}, f32[2048]{0:T(1024)S(1)}, f32[2048]{0:T(1024)S(1)}) all-reduce(f32[2048]{0:T(1024)S(1)} %dynamic-update-slice, f32[2048]{0:T(1024)S(1)} %dynamic-update-slice.1, f32[2048]{0:T(1024)S(1)} %dynamic-update-slice.2), channel_id=2, replica_groups=mesh['heads'=4,'batch'=8] {'heads','batch'}, use_global_device_ids=true, to_apply=%add | all-reduce | flops 6144 | bytes 49152
  133.8 0.1 reshape.81
  133.9 0.1 reshape.82
  134.0 0.1 reshape.83
  134.1 1.4 %while.19 = (s32[]{:T(128)}, f32[64]{0:T(128)S(1)}, f32[64]{0:T(128)S(1)}, f32[64]{0:T(128)S(1)}, f32[32,64]{1,0:T(8,128)S(1)}, /*index=5*/f32[32,64]{1,0:T(8,12...) while((s32[]{:T(128)}, f32[64]{0:T(128)S(1)}, f32[64]{0:T(128)S(1)}, f32[64]{0:T(128)S(1)}, ...), condition=%wide.region_10.11_spmd, body=%wide.region_9.10_spmd.sunk | while | flops 453 | bytes 2451 | solution.py:15
  135.5 0.6 dynamic_slice.46
  (71 shorter events, 1.2 us)
Async XLA Ops:
  7.2 86.6 %copy-start = (bf16[4096,128]{1,0:T(8,128)(2,1)S(1)}, bf16[4096,128]{1,0:T(8,128)(2,1)}, u32[]{:S(2)}) copy-start(bf16[4096,128]{1,0:T(8,128)(2,1)} %param.30) | copy-start | bytes 3145732
  7.2 52.6 %all-reduce.6.cloned.1.call-start = ((), (), s32[]{:S(2)}) async-start(), calls=%async_computation | async-start | bytes 262144 | tf_op jit(solution)/shard_map/psum | solution.py:80
  7.2 8.4 %copy-start.1 = (f32[8,8,128,128]{3,2,1,0:T(8,128)S(1)}, f32[8,8,128,128]{3,2,1,0:T(8,128)}, u32[]{:S(2)}) copy-start(f32[8,8,128,128]{3,2,1,0:T(8,128)} %param.24) | copy-start | bytes 12582916
  10.2 9.1 %copy-start.7 = (f32[8,8]{1,0:T(8,128)S(1)}, f32[8,8]{1,0:T(8,128)}, u32[]{:S(2)}) copy-start(f32[8,8]{1,0:T(8,128)} %param.22) | copy-start | bytes 772
  10.3 9.1 %copy-start.10 = (f32[8]{0:T(128)S(1)}, f32[8]{0:T(128)}, u32[]{:S(2)}) copy-start(f32[8]{0:T(128)} %param.23) | copy-start | bytes 100
  10.3 9.1 %copy-start.8 = (f32[8,8]{1,0:T(8,128)S(1)}, f32[8,8]{1,0:T(8,128)}, u32[]{:S(2)}) copy-start(f32[8,8]{1,0:T(8,128)} %param.21) | copy-start | bytes 772
  10.3 9.2 %copy-start.3 = (bf16[8,1024]{1,0:T(8,128)(2,1)S(1)}, bf16[8,1024]{1,0:T(8,128)(2,1)}, u32[]{:S(2)}) copy-start(bf16[8,1024]{1,0:T(8,128)(2,1)} %param.19) | copy-start | bytes 49156
  10.3 9.4 %copy-start.5 = (bf16[8,1024]{1,0:T(8,128)(2,1)S(1)}, bf16[8,1024]{1,0:T(8,128)(2,1)}, u32[]{:S(2)}) copy-start(bf16[8,1024]{1,0:T(8,128)(2,1)} %param.20) | copy-start | bytes 49156
  10.3 9.4 %copy-start.9 = (f32[128]{0:T(128)S(1)}, f32[128]{0:T(128)}, u32[]{:S(2)}) copy-start(f32[128]{0:T(128)} %param.25) | copy-start | bytes 1540
  19.7 5.4 %copy-start.11 = (s32[64]{0:T(128)S(1)}, s32[64]{0:T(128)}, u32[]{:S(2)}) copy-start(s32[64]{0:T(128)} %param.31) | copy-start | bytes 772
  19.7 40.0 %copy-start.2 = (bf16[8,4096]{1,0:T(8,128)(2,1)S(1)}, bf16[8,4096]{1,0:T(8,128)(2,1)}, u32[]{:S(2)}) copy-start(bf16[8,4096]{1,0:T(8,128)(2,1)} %param.27) | copy-start | bytes 196612
  19.7 40.0 %copy-start.4 = (f32[4096]{0:T(1024)S(1)}, f32[4096]{0:T(1024)}, u32[]{:S(2)}) copy-start(f32[4096]{0:T(1024)} %param.28) | copy-start | bytes 49156
  19.7 40.0 %copy-start.6 = (f32[4096]{0:T(1024)S(1)}, f32[4096]{0:T(1024)}, u32[]{:S(2)}) copy-start(f32[4096]{0:T(1024)} %param.29) | copy-start | bytes 49156
Sparse Core Ops, SparseCore 0:
  25.2 34.4 all-reduce.5
where the time goes:
time: 144 us; the launch traced here: 143 us
  blocking collectives  70.1 us (49%)
  waiting for transfers between devices  34.6 us (24%)
  matrix products  14.7 us (10%)
  between operations  14.2 us (10%)
  other arithmetic  6.89 us (5%)
  local copies, waits for them, and re-layouts  1.82 us (1%)
    unnamed x1, blocking collectives  38.7 us
    psum x1, waiting for transfers between devices, per_device(): attn = lax.psum(partial_out, 'heads')  34.6 us
    all_gather x1, blocking collectives, per_device(): lax.all_gather(normed, 'batch', axis=0, tiled=True)  31.4 us
    dot_general x1, matrix products, head_outputs(): jnp.einsum('bhk,bhkv->bhv', key_n, state, precision=lax.Precision.HIGHEST)  5.31 us
    dot_general x1, matrix products, per_device(): partial_out = jnp.dot(headout, out_proj, preferred_element_type=jnp.float32)  5.31 us
    dot_general x1, matrix products, head_outputs(): jnp.einsum('bhk,bhkv->bhv', query_n, state, precision=lax.Precision.HIGHEST)  3.66 us
  transfers between devices with their start and end apart: 1, of which 1 were waited for; matrix products, arithmetic and copies ran while one was open for 0% of the time, Pallas kernels for 0%

commit v1 on v0

--- a/solution.py
+++ b/solution.py
@@ -77,7 +77,9 @@
     )
     partial_out = jnp.dot(headout, out_proj, preferred_element_type=jnp.float32)
     rows_own = residual.shape[0]
-    attn = lax.psum(partial_out, "heads")
+    attn = partial_out
+    for hop in (1, 2):
+        attn = attn + lax.ppermute(attn, "heads", [(dev, dev ^ hop) for dev in range(4)])
     hsum = residual.astype(jnp.float32) + attn
     rstd = 1.0 / jnp.sqrt(jnp.mean(hsum * hsum, axis=1) + epsilon)
     value = rstd * jnp.sum(hsum * final_gain * value_weight, axis=1)

time: 144 us -> 103 us (0.72)
  waiting for transfers between devices: 34.6 us -> 4.79 us
  between operations: 14.2 us -> 0.83 us
  starting transfers between devices: 0.04 us -> 3.43 us
  other arithmetic: 6.89 us -> 5.12 us
    psum x1 -> x0, waiting for transfers between devices: 34.6 us -> none  [per_device(): attn = lax.psum(partial_out, 'heads')]
    ppermute x0 -> x2, waiting for transfers between devices: none -> 4.79 us  [per_device(): lax.ppermute(attn, 'heads', [(dev, dev ^ hop) for dev in range(4)])]
    ppermute x0 -> x2, starting transfers between devices: none -> 3.43 us  [per_device(): lax.ppermute(attn, 'heads', [(dev, dev ^ hop) for dev in range(4)])]
  transfers between devices with their start and end apart: 1 -> 2, of which waited for: 1 -> 2; matrix products, arithmetic and copies ran while one was open for 0% -> 0% of each run, Pallas kernels for 0% -> 0%
where the time goes in v1:
time: 103 us; the launch traced here: 102 us
  blocking collectives  71.5 us (69%)
  matrix products  14 us (14%)
  other arithmetic  5.12 us (5%)
  waiting for transfers between devices  4.79 us (5%)
  starting transfers between devices  3.43 us (3%)
  local copies, waits for them, and re-layouts  1.82 us (2%)
    unnamed x1, blocking collectives  39.5 us
    all_gather x1, blocking collectives, per_device(): lax.all_gather(normed, 'batch', axis=0, tiled=True)  32 us
    dot_general x1, matrix products, head_outputs(): jnp.einsum('bhk,bhkv->bhv', key_n, state, precision=lax.Precision.HIGHEST)  5.31 us
    ppermute x2, waiting for transfers between devices, per_device(): lax.ppermute(attn, 'heads', [(dev, dev ^ hop) for dev in range(4)])  4.79 us
    dot_general x1, matrix products, per_device(): partial_out = jnp.dot(headout, out_proj, preferred_element_type=jnp.float32)  4.65 us
    dot_general x1, matrix products, head_outputs(): jnp.einsum('bhk,bhkv->bhv', query_n, state, precision=lax.Precision.HIGHEST)  3.66 us
    ppermute x2, starting transfers between devices, per_device(): lax.ppermute(attn, 'heads', [(dev, dev ^ hop) for dev in range(4)])  3.43 us
  transfers between devices with their start and end apart: 2, of which 2 were waited for; matrix products, arithmetic and copies ran while one was open for 0% of the time, Pallas kernels for 0%

profile of v1, /device:TPU:0, one launch (start us, length us, event | category | flops | bytes accessed | tf_op | source)
XLA Modules:
  0.0 102.1 jit_solution(7401566609361369546)
XLA Ops:
  0.7 1.0 fusion.7
  1.6 1.1 %fusion.9 = f32[8,8]{0,1:T(8,128)S(1)} fusion(bf16[8,1024]{1,0:T(8,128)(2,1)} %param.18), kind=kLoop, calls=%fused_computation.22 | loop fusion | flops 24512 | bytes 16640 | tf_op jit(solution)/shard_map/reduce_sum | solution.py:31
  2.8 0.9 fusion.22
  3.7 5.3 %fusion.16 = f32[8,8,1,128]{3,2,1,0:T(1,128)S(1)} fusion(f32[8,8,128,128]{3,2,1,0:T(8,128)} %param.24, f32[8,8,128,1]{2,0,1,3:T(8,128)S(1)} %get-tuple-element.210), kind=kOutput, calls=%fused_computation.32 | convolution fusion | flops 12582912 | bytes 4259840 | tf_op jit(solution)/shard_map/bhk,bhkv->bhv/dot_general | solution.py:35
  9.1 3.7 %fusion.18 = f32[8,8,1,128]{3,2,1,0:T(1,128)S(1)} fusion(f32[8,8,128,128]{3,2,1,0:T(8,128)S(1)} %copy-done.1, f32[8,8,128,1]{2,0,1,3:T(8,128)S(1)} %get-tuple-element.208), kind=kOutput, calls=%fused_computation.34 | convolution fusion | flops 12582912 | bytes 4259840 | tf_op jit(solution)/shard_map/bhk,bhkv->bhv/dot_general | solution.py:34
  12.8 0.1 copy.19
  12.9 0.2 multiply_reduce_fusion.2
  13.2 4.6 %fusion.23 = f32[8,4096]{1,0:T(8,128)S(1)} fusion(bf16[1024,4096]{1,0:T(8,128)(2,1)} %param.26, bf16[8,1024]{1,0:T(8,128)(2,1)S(1)} %copy-done.5, f32[128]{0:T(128)S(1)} %copy-done.9, f32[8,8]{0,1:T(8,128)S(1)} %add_sqrt_fusion, f32[8,8,1,128]{3,2,1,0:T(1,128)S(1)} %fusion.16, f32[8,8,1,128]{3,2,1,0:T(1,128)S(1)} %fusion.18, ...), kind=kOutput, calls=%fused_computation.44 | convolution fusion | flops 67231744 | bytes 8619264 | tf_op jit(solution)/shard_map/dot_general | solution.py:78
  17.8 0.5 collective-permute-start
  18.3 1.0 collective-permute-done
  19.3 2.9 %collective-permute-start.1 = (f32[8,4096]{1,0:T(8,128)S(1)}, f32[8,4096]{1,0:T(8,128)S(1)}, u32[]{:S(2)}, u32[]{:S(2)}) collective-permute-start(f32[8,4096]{1,0:T(8,128)S(1)} %add.129), channel_id=1, source_target_pairs={{0,16},{8,24},{16,0},{24,8},{1,17},{9,25},{17,1},{25,9},{2,18},{10... | collective-permute-start | bytes 393224 | tf_op jit(solution)/shard_map/ppermute | solution.py:82
  22.3 3.8 %collective-permute-done.1 = f32[8,4096]{1,0:T(8,128)S(1)} collective-permute-done((f32[8,4096]{1,0:T(8,128)S(1)}, f32[8,4096]{1,0:T(8,128)S(1)}, u32[]{:S(2)}, u32[]{:S(2)}) %collective-permute-start.1) | collective-permute-done | bytes 131104 | tf_op jit(solution)/shard_map/ppermute | solution.py:82
  26.1 0.2 multiply_reduce_fusion
  26.3 0.5 fusion.32
  26.8 0.1 multiply_convert_fusion
  26.9 32.0 %all_gather.21 = bf16[64,4096]{1,0:T(8,128)(2,1)S(1)} all-gather(bf16[8,4096]{1,0:T(8,128)(2,1)S(1)} %multiply_convert_fusion), channel_id=1, replica_groups=mesh['heads'=4,'batch'=8] {'batch'}, dimensions={0}, use_global_device_ids=true | all-gather | bytes 589824 | tf_op jit(solution)/shard_map/all_gather | solution.py:88
  58.9 0.4 fusion.35
  59.3 0.2 select_reduce_fusion
  59.5 0.3 dynamic-update-slice
  59.8 0.3 dynamic-update-slice.2
  60.0 0.3 dynamic-update-slice.1
  60.3 39.5 %all-reduce.3 = (f32[2048]{0:T(1024)S(1)}, f32[2048]{0:T(1024)S(1)}, f32[2048]{0:T(1024)S(1)}) all-reduce(f32[2048]{0:T(1024)S(1)} %dynamic-update-slice, f32[2048]{0:T(1024)S(1)} %dynamic-update-slice.1, f32[2048]{0:T(1024)S(1)} %dynamic-update-slice.2), channel_id=2, replica_groups=mesh['heads'=4,'batch'=8] {'heads','batch'}, use_global_device_ids=true, to_apply=%add | all-reduce | flops 6144 | bytes 49152
  100.1 1.4 %while.19 = (s32[]{:T(128)}, f32[64]{0:T(128)S(1)}, f32[64]{0:T(128)S(1)}, f32[64]{0:T(128)S(1)}, f32[32,64]{1,0:T(8,128)S(1)}, /*index=5*/f32[32,64]{1,0:T(8,12...) while((s32[]{:T(128)}, f32[64]{0:T(128)S(1)}, f32[64]{0:T(128)S(1)}, f32[64]{0:T(128)S(1)}, ...), condition=%wide.region_9.10_spmd, body=%wide.region_8.9_spmd.sunk | while | flops 453 | bytes 2451 | solution.py:15
  101.5 0.6 dynamic_slice.46
  (73 shorter events, 1.3 us)
Async XLA Ops:
  0.6 58.2 %copy-start = (bf16[4096,128]{1,0:T(8,128)(2,1)S(1)}, bf16[4096,128]{1,0:T(8,128)(2,1)}, u32[]{:S(2)}) copy-start(bf16[4096,128]{1,0:T(8,128)(2,1)} %param.30) | copy-start | bytes 3145732
  0.6 8.4 %copy-start.1 = (f32[8,8,128,128]{3,2,1,0:T(8,128)S(1)}, f32[8,8,128,128]{3,2,1,0:T(8,128)}, u32[]{:S(2)}) copy-start(f32[8,8,128,128]{3,2,1,0:T(8,128)} %param.24) | copy-start | bytes 12582916
  3.7 9.1 %copy-start.7 = (f32[8,8]{1,0:T(8,128)S(1)}, f32[8,8]{1,0:T(8,128)}, u32[]{:S(2)}) copy-start(f32[8,8]{1,0:T(8,128)} %param.22) | copy-start | bytes 772
  3.7 9.1 %copy-start.10 = (f32[8]{0:T(128)S(1)}, f32[8]{0:T(128)}, u32[]{:S(2)}) copy-start(f32[8]{0:T(128)} %param.23) | copy-start | bytes 100
  3.7 9.1 %copy-start.8 = (f32[8,8]{1,0:T(8,128)S(1)}, f32[8,8]{1,0:T(8,128)}, u32[]{:S(2)}) copy-start(f32[8,8]{1,0:T(8,128)} %param.21) | copy-start | bytes 772
  3.7 9.2 %copy-start.2 = (bf16[8,1024]{1,0:T(8,128)(2,1)S(1)}, bf16[8,1024]{1,0:T(8,128)(2,1)}, u32[]{:S(2)}) copy-start(bf16[8,1024]{1,0:T(8,128)(2,1)} %param.19) | copy-start | bytes 49156
  3.7 9.4 %copy-start.5 = (bf16[8,1024]{1,0:T(8,128)(2,1)S(1)}, bf16[8,1024]{1,0:T(8,128)(2,1)}, u32[]{:S(2)}) copy-start(bf16[8,1024]{1,0:T(8,128)(2,1)} %param.20) | copy-start | bytes 49156
  3.7 9.4 %copy-start.9 = (f32[128]{0:T(128)S(1)}, f32[128]{0:T(128)}, u32[]{:S(2)}) copy-start(f32[128]{0:T(128)} %param.25) | copy-start | bytes 1540
  13.1 9.1 %copy-start.11 = (s32[64]{0:T(128)S(1)}, s32[64]{0:T(128)}, u32[]{:S(2)}) copy-start(s32[64]{0:T(128)} %param.31) | copy-start | bytes 772
  13.1 12.9 %copy-start.3 = (bf16[8,4096]{1,0:T(8,128)(2,1)S(1)}, bf16[8,4096]{1,0:T(8,128)(2,1)}, u32[]{:S(2)}) copy-start(bf16[8,4096]{1,0:T(8,128)(2,1)} %param.27) | copy-start | bytes 196612
  13.1 12.9 %copy-start.4 = (f32[4096]{0:T(1024)S(1)}, f32[4096]{0:T(1024)}, u32[]{:S(2)}) copy-start(f32[4096]{0:T(1024)} %param.28) | copy-start | bytes 49156
  13.2 12.9 %copy-start.6 = (f32[4096]{0:T(1024)S(1)}, f32[4096]{0:T(1024)}, u32[]{:S(2)}) copy-start(f32[4096]{0:T(1024)} %param.29) | copy-start | bytes 49156
  17.8 1.5 %collective-permute-start = (f32[8,4096]{1,0:T(8,128)S(1)}, f32[8,4096]{1,0:T(8,128)S(1)}, u32[]{:S(2)}, u32[]{:S(2)}) collective-permute-start(f32[8,4096]{1,0:T(8,128)S(1)} %fusion.23), channel_id=1, source_target_pairs={{0,8},{8,0},{16,24},{24,16},{1,9},{9,1},{17,25},{25,17},{2,10},{10... | collective-permute-start | bytes 393224 | tf_op jit(solution)/shard_map/ppermute | solution.py:82
  19.3 6.7 %collective-permute-start.1 = (f32[8,4096]{1,0:T(8,128)S(1)}, f32[8,4096]{1,0:T(8,128)S(1)}, u32[]{:S(2)}, u32[]{:S(2)}) collective-permute-start(f32[8,4096]{1,0:T(8,128)S(1)} %add.129), channel_id=1, source_target_pairs={{0,16},{8,24},{16,0},{24,8},{1,17},{9,25},{17,1},{25,9},{2,18},{10... | collective-permute-start | bytes 393224 | tf_op jit(solution)/shard_map/ppermute | solution.py:82
